TPU v7x, 32 devices: a whole 2x2x4 slice. The times are simulated.
32 devices in a mesh: wide: 8 (over y, x, core), narrow: 4 (over z).
Axes of the slice: x: 2, y: 2, z: 4, core: 2. Of those that a mesh axis runs over, the one named last changes fastest.
Arguments:
- layer_input: bfloat16 [4, 2048, 2048], P(None, 'wide'), may hold values from -6 to 6
- grad_out: bfloat16 [4, 2048, 2048], P(None, 'wide'), may hold values from -6 to 6
- lengths: int32 [4, 8], replicated, may hold values from 1 to 1024, 2048 in all within a row
- w_query: bfloat16 [2048, 2048], P('wide', 'narrow'), may hold values from -0.125 to 0.125
- w_key: bfloat16 [2048, 1024], P('wide', 'narrow'), may hold values from -0.125 to 0.125
- w_value: bfloat16 [2048, 1024], P('wide', 'narrow'), may hold values from -0.125 to 0.125
- w_out: bfloat16 [2048, 2048], P('narrow', 'wide'), may hold values from -0.75 to 0.75
- w_gate: bfloat16 [2048, 6144], P('wide', 'narrow'), may hold values from -0.125 to 0.125
- w_up: bfloat16 [2048, 6144], P('wide', 'narrow'), may hold values from -0.125 to 0.125
- w_down: bfloat16 [6144, 2048], P('narrow', 'wide'), may hold values from -0.078125 to 0.078125
- gain_attn: float32 [2048], replicated, may hold values from 0.25 to 1.75
- gain_ffn: float32 [2048], replicated, may hold values from 0.25 to 1.75
- gain_query: float32 [128], replicated, may hold values from 0.25 to 1.75
- gain_key: float32 [128], replicated, may hold values from 0.25 to 1.75
Outputs:
- output: bfloat16 [4, 2048, 2048], P(None, 'wide')
- grad_input: float32 [4, 2048, 2048], P(None, 'wide')
- grad_wquery: float32 [2048, 2048], P('wide', 'narrow')
- grad_wkey: float32 [2048, 1024], P('wide', 'narrow')
- grad_wvalue: float32 [2048, 1024], P('wide', 'narrow')
- grad_wout: float32 [2048, 2048], P('narrow', 'wide')
- grad_wgate: float32 [2048, 6144], P('wide', 'narrow')
- grad_wup: float32 [2048, 6144], P('wide', 'narrow')
- grad_wdown: float32 [6144, 2048], P('narrow', 'wide')
- grad_gattn: float32 [2048], replicated
- grad_gffn: float32 [2048], replicated
- grad_gquery: float32 [128], replicated
- grad_gkey: float32 [128], replicated
Inputs may be any that keep to these rules, and one draw needn't show every extreme that they name: `lengths`: each row cuts the 2048 tokens of its micro-batch into 8 consecutive pieces in order; pieces 0 to 6 are documents and the last piece is padding. A row's pieces sum to 2048, and its largest piece is exactly 1024.
All inputs are finite; a program needn't handle non-finite values.
Results may differ from a plain program's by a relative error of at most 0.022.
Values may be sent and summed in bfloat16 or wider, within the bound.
A program may use at most 256 MiB of HBM per device.

v0:
```python
import math
import jax
import jax.numpy as jnp
from jax import lax
from jax.sharding import PartitionSpec as P

HD = 128
NDOC = 8
EPSILON = 1e-06
THETA = 1000000.0


def rms_norm(values, gain):
    return values * lax.rsqrt(jnp.mean(values * values, axis=-1, keepdims=True) + EPSILON) * gain


def unit_rows(values):
    return values * lax.rsqrt(jnp.mean(values * values, axis=-1, keepdims=True) + EPSILON)


def rotate(values, cosine, sine):
    midway = values.shape[-1] // 2
    turned = jnp.concatenate([-values[..., midway:], values[..., :midway]], axis=-1)
    return values * cosine + turned * sine


def layout(lengths_row, total):
    finish = jnp.cumsum(lengths_row)
    starts = finish - lengths_row
    places = jnp.arange(total, dtype=jnp.int32)
    segment = jnp.sum((places[:, None] >= finish[None, :]).astype(jnp.int32), axis=1)
    member = segment[:, None] == jnp.arange(finish.shape[0], dtype=jnp.int32)[None, :]
    opening = jnp.sum(jnp.where(member, starts[None, :], 0), axis=1)
    return (segment, places - opening)


def angles(place):
    frequency = jnp.exp(-math.log(THETA) * jnp.arange(0, HD, 2).astype(jnp.float32) / HD)
    turning = place.astype(jnp.float32)[:, None] * frequency[None, :]
    turning = jnp.concatenate([turning, turning], axis=-1)
    return (jnp.cos(turning), jnp.sin(turning))


def allowed(query_seg, query_idx, key_seg, key_idx):
    same_doc = query_seg[:, None] == key_seg[None, :]
    causal = key_idx[None, :] <= query_idx[:, None]
    usable = (key_seg[None, :] != NDOC - 1) | (key_idx[None, :] == query_idx[:, None])
    return same_doc & causal & usable


def attention_scores(query_low, key_all, mask_local, factor):
    scores = (
        jnp.einsum("tgrd,kgd->grtk", query_low, key_all, preferred_element_type=jnp.float32)
        * factor
    )
    return jnp.where(mask_local[None, None], scores, -1e30)


def one_batch(row_input, grad_row, lengths_row, gathered, gains):
    w_query, w_key, w_value, w_out, w_gate, w_up, w_down = gathered
    gain_attn, gain_ffn, gain_query, gain_key = gains
    tok_rows = row_input.shape[0]
    total = tok_rows * lax.axis_size("wide")
    groups = w_key.shape[1] // HD
    repeat = w_query.shape[1] // w_key.shape[1]
    factor = 1.0 / math.sqrt(HD)
    first_row = lax.axis_index("wide") * tok_rows
    segment, place = layout(lengths_row, total)
    positions = jnp.arange(total, dtype=jnp.int32)
    query_seg = lax.dynamic_slice_in_dim(segment, first_row, tok_rows)
    query_idx = lax.dynamic_slice_in_dim(positions, first_row, tok_rows)
    mask_local = allowed(query_seg, query_idx, segment, positions)
    cosine, sine = angles(lax.dynamic_slice_in_dim(place, first_row, tok_rows))

    def head_norm(rows, gain):
        return rotate(rms_norm(rows, gain), cosine[:, None, :], sine[:, None, :])

    input_float = row_input.astype(jnp.float32)
    grad_float = grad_row.astype(jnp.float32)
    normed_one, pull_one = jax.vjp(lambda rows: rms_norm(rows, gain_attn), input_float)
    hidden_one = normed_one.astype(jnp.bfloat16)
    query_raw = jnp.dot(hidden_one, w_query, preferred_element_type=jnp.float32).reshape(
        tok_rows, groups * repeat, HD
    )
    key_raw = jnp.dot(hidden_one, w_key, preferred_element_type=jnp.float32).reshape(
        tok_rows, groups, HD
    )
    value_low = jnp.dot(hidden_one, w_value, preferred_element_type=jnp.float32).astype(
        jnp.bfloat16
    )
    query_turned, pull_query = jax.vjp(head_norm, query_raw, gain_query)
    key_turned, pull_key = jax.vjp(head_norm, key_raw, gain_key)
    query_low = query_turned.astype(jnp.bfloat16).reshape(tok_rows, groups, repeat, HD)
    key_low = key_turned.astype(jnp.bfloat16).reshape(tok_rows, groups * HD)
    key_all, value_all = (
        lax.all_gather(key_low, "wide", axis=0, tiled=True),
        lax.all_gather(value_low, "wide", axis=0, tiled=True),
    )
    key_all = key_all.reshape(total, groups, HD)
    value_all = value_all.reshape(total, groups, HD)
    scores = attention_scores(query_low, key_all, mask_local, factor)
    highest = jnp.max(scores, axis=-1, keepdims=True)
    exponent = jnp.exp(scores - highest)
    denominator = jnp.sum(exponent, axis=-1, keepdims=True)
    log_total = highest + jnp.log(denominator)
    probs_low = (exponent / denominator).astype(jnp.bfloat16)
    mixed = jnp.einsum("grtk,kgd->tgrd", probs_low, value_all, preferred_element_type=jnp.float32)
    mixed_low = mixed.reshape(tok_rows, groups * repeat * HD).astype(jnp.bfloat16)
    attn_part = jnp.dot(mixed_low, w_out, preferred_element_type=jnp.float32)
    middle = input_float + lax.psum(attn_part.astype(jnp.bfloat16), "narrow").astype(jnp.float32)
    normed_two, pull_two = jax.vjp(lambda rows: rms_norm(rows, gain_ffn), middle)
    hidden_two = normed_two.astype(jnp.bfloat16)
    unit_two = unit_rows(middle)
    gate = jnp.dot(hidden_two, w_gate, preferred_element_type=jnp.float32)
    up_proj = jnp.dot(hidden_two, w_up, preferred_element_type=jnp.float32)
    active, pull_active = jax.vjp(
        lambda gate_in, up_in: jax.nn.silu(gate_in) * up_in, gate, up_proj
    )
    active_low = active.astype(jnp.bfloat16)
    ffn_part = jnp.dot(active_low, w_down, preferred_element_type=jnp.float32)
    output_low = (
        middle + lax.psum(ffn_part.astype(jnp.bfloat16), "narrow").astype(jnp.float32)
    ).astype(jnp.bfloat16)
    grad_wdown = jnp.einsum("tf,td->fd", active_low, grad_row, preferred_element_type=jnp.float32)
    grad_active = jnp.einsum("td,fd->tf", grad_row, w_down, preferred_element_type=jnp.float32)
    grad_gate, grad_upper = pull_active(grad_active)
    gate_back = grad_gate.astype(jnp.bfloat16)
    upper_back = grad_upper.astype(jnp.bfloat16)
    grad_wgate = jnp.einsum("td,tf->df", hidden_two, gate_back, preferred_element_type=jnp.float32)
    grad_wup = jnp.einsum("td,tf->df", hidden_two, upper_back, preferred_element_type=jnp.float32)
    partial_two = jnp.einsum(
        "tf,df->td", gate_back, w_gate, preferred_element_type=jnp.float32
    ) + jnp.einsum("tf,df->td", upper_back, w_up, preferred_element_type=jnp.float32)
    gain_two = jnp.sum(partial_two * unit_two, axis=0)
    grad_middle = (
        grad_float
        + pull_two(lax.psum(partial_two.astype(jnp.bfloat16), "narrow").astype(jnp.float32))[0]
    )
    middle_low = grad_middle.astype(jnp.bfloat16)
    grad_wout = jnp.einsum("th,td->hd", mixed_low, middle_low, preferred_element_type=jnp.float32)
    grad_mixed = jnp.einsum("td,hd->th", middle_low, w_out, preferred_element_type=jnp.float32)
    grad_mixed = grad_mixed.astype(jnp.bfloat16).reshape(tok_rows, groups, repeat, HD)
    scores = attention_scores(query_low, key_all, mask_local, factor)
    probs = jnp.exp(scores - log_total)
    grad_probs = jnp.einsum(
        "tgrd,kgd->grtk", grad_mixed, value_all, preferred_element_type=jnp.float32
    )
    weighted = jnp.sum(probs * grad_probs, axis=-1, keepdims=True)
    grad_scores = (probs * (grad_probs - weighted)).astype(jnp.bfloat16)
    grad_turned = (
        jnp.einsum("grtk,kgd->tgrd", grad_scores, key_all, preferred_element_type=jnp.float32)
        * factor
    )
    grad_keyall = (
        jnp.einsum("grtk,tgrd->kgd", grad_scores, query_low, preferred_element_type=jnp.float32)
        * factor
    )
    grad_valueall = jnp.einsum(
        "grtk,tgrd->kgd", probs.astype(jnp.bfloat16), grad_mixed, preferred_element_type=jnp.float32
    )
    grad_keys, grad_values = (
        lax.psum_scatter(
            grad_keyall.reshape(total, groups * HD).astype(jnp.bfloat16),
            "wide",
            scatter_dimension=0,
            tiled=True,
        ).astype(jnp.float32),
        lax.psum_scatter(
            grad_valueall.reshape(total, groups * HD).astype(jnp.bfloat16),
            "wide",
            scatter_dimension=0,
            tiled=True,
        ).astype(jnp.float32),
    )
    grad_qraw, gain_q = pull_query(grad_turned.reshape(tok_rows, groups * repeat, HD))
    grad_kraw, gain_k = pull_key(grad_keys.reshape(tok_rows, groups, HD))
    query_back = grad_qraw.reshape(tok_rows, groups * repeat * HD).astype(jnp.bfloat16)
    key_back = grad_kraw.reshape(tok_rows, groups * HD).astype(jnp.bfloat16)
    value_back = grad_values.astype(jnp.bfloat16)
    grad_wquery = jnp.einsum(
        "td,th->dh", hidden_one, query_back, preferred_element_type=jnp.float32
    )
    grad_wkey = jnp.einsum("td,th->dh", hidden_one, key_back, preferred_element_type=jnp.float32)
    grad_wvalue = jnp.einsum(
        "td,th->dh", hidden_one, value_back, preferred_element_type=jnp.float32
    )
    partial_one = (
        jnp.einsum("th,dh->td", query_back, w_query, preferred_element_type=jnp.float32)
        + jnp.einsum("th,dh->td", key_back, w_key, preferred_element_type=jnp.float32)
        + jnp.einsum("th,dh->td", value_back, w_value, preferred_element_type=jnp.float32)
    )
    gain_one = jnp.sum(partial_one * unit_rows(input_float), axis=0)
    grad_input = (
        grad_middle
        + pull_one(lax.psum(partial_one.astype(jnp.bfloat16), "narrow").astype(jnp.float32))[0]
    )
    weight_grads = (
        grad_wquery,
        grad_wkey,
        grad_wvalue,
        grad_wout,
        grad_wgate,
        grad_wup,
        grad_wdown,
    )
    return (output_low, grad_input, weight_grads, (gain_one, gain_two, gain_q, gain_k))


def local(
    layer_input,
    grad_out,
    lengths,
    w_query,
    w_key,
    w_value,
    w_out,
    w_gate,
    w_up,
    w_down,
    gain_attn,
    gain_ffn,
    gain_query,
    gain_key,
):
    width = lax.axis_size("wide")
    shards = (w_query, w_key, w_value, w_out, w_gate, w_up, w_down)
    along_rows = (True, True, True, False, True, True, False)
    gains = (gain_attn, gain_ffn, gain_query, gain_key)
    totals = tuple(
        (
            jnp.zeros(
                (
                    (piece.shape[0] * width, piece.shape[1])
                    if rows_first
                    else (piece.shape[0], piece.shape[1] * width)
                ),
                jnp.float32,
            )
            for piece, rows_first in zip(shards, along_rows)
        )
    )
    gain_terms = tuple((jnp.zeros(gain.shape, jnp.float32) for gain in gains))
    outputs = []
    grad_inputs = []
    for micro in range(layer_input.shape[0]):
        gathered = (
            lax.all_gather(w_query, "wide", axis=0, tiled=True),
            lax.all_gather(w_key, "wide", axis=0, tiled=True),
            lax.all_gather(w_value, "wide", axis=0, tiled=True),
            lax.all_gather(w_out, "wide", axis=1, tiled=True),
            lax.all_gather(w_gate, "wide", axis=0, tiled=True),
            lax.all_gather(w_up, "wide", axis=0, tiled=True),
            lax.all_gather(w_down, "wide", axis=1, tiled=True),
        )
        output, grad_input, weight_grads, gain_grads = one_batch(
            layer_input[micro], grad_out[micro], lengths[micro], gathered, gains
        )
        outputs.append(output)
        grad_inputs.append(grad_input)
        gain_terms = tuple((running + fresh for running, fresh in zip(gain_terms, gain_grads)))
        totals = tuple((running + fresh for running, fresh in zip(totals, weight_grads)))
    results = (
        lax.psum_scatter(
            totals[0].astype(jnp.bfloat16), "wide", scatter_dimension=0, tiled=True
        ).astype(jnp.float32),
        lax.psum_scatter(
            totals[1].astype(jnp.bfloat16), "wide", scatter_dimension=0, tiled=True
        ).astype(jnp.float32),
        lax.psum_scatter(
            totals[2].astype(jnp.bfloat16), "wide", scatter_dimension=0, tiled=True
        ).astype(jnp.float32),
        lax.psum_scatter(
            totals[3].astype(jnp.bfloat16), "wide", scatter_dimension=1, tiled=True
        ).astype(jnp.float32),
        lax.psum_scatter(
            totals[4].astype(jnp.bfloat16), "wide", scatter_dimension=0, tiled=True
        ).astype(jnp.float32),
        lax.psum_scatter(
            totals[5].astype(jnp.bfloat16), "wide", scatter_dimension=0, tiled=True
        ).astype(jnp.float32),
        lax.psum_scatter(
            totals[6].astype(jnp.bfloat16), "wide", scatter_dimension=1, tiled=True
        ).astype(jnp.float32),
    )
    gain_total = lax.psum(gain_terms, ("wide", "narrow"))
    return (
        jnp.stack(outputs),
        jnp.stack(grad_inputs),
        results[0],
        results[1],
        results[2],
        results[3],
        results[4],
        results[5],
        results[6],
        gain_total[0],
        gain_total[1],
        gain_total[2],
        gain_total[3],
    )


def solution(mesh):
    in_specs = (
        P(None, "wide", None),
        P(None, "wide", None),
        P(),
        P("wide", "narrow"),
        P("wide", "narrow"),
        P("wide", "narrow"),
        P("narrow", "wide"),
        P("wide", "narrow"),
        P("wide", "narrow"),
        P("narrow", "wide"),
        P(),
        P(),
        P(),
        P(),
    )
    out_specs = (
        P(None, "wide", None),
        P(None, "wide", None),
        P("wide", "narrow"),
        P("wide", "narrow"),
        P("wide", "narrow"),
        P("narrow", "wide"),
        P("wide", "narrow"),
        P("wide", "narrow"),
        P("narrow", "wide"),
        P(),
        P(),
        P(),
        P(),
    )
    return jax.shard_map(local, mesh=mesh, in_specs=in_specs, out_specs=out_specs, check_vma=False)
```

profile of v0, /device:TPU:0, one launch (start us, length us, event | category | flops | bytes accessed | tf_op | source)
XLA Modules:
  0.0 1960.0 jit_solution(11782084816646856816)
XLA Ops:
  14.2 21.9 %all-gather.16.cloned.1.call-done = bf16[2048,256]{1,0:T(8,128)(2,1)} async-done(((bf16[256,256]{1,0:T(8,128)(2,1)}), bf16[2048,256]{1,0:T(8,128)(2,1)}) %all-gather.16.cloned.1.call-update) | async-done | bytes 1048592 | tf_op jit(solution)/shard_map/all_gather | solution.py:249
  39.5 21.8 %all-gather.20.cloned.1.call-done = bf16[2048,256]{1,0:T(8,128)(2,1)} async-done(((bf16[256,256]{1,0:T(8,128)(2,1)}), bf16[2048,256]{1,0:T(8,128)(2,1)}) %all-gather.20.cloned.1.call-update) | async-done | bytes 1048592 | tf_op jit(solution)/shard_map/all_gather | solution.py:248
  72.1 18.9 all-gather.24.cloned.1.call-done
  94.9 21.8 %all-gather.38.cloned.1.call-done = bf16[2048,256]{1,0:T(8,128)(2,1)} async-done(((bf16[256,256]{1,0:T(8,128)(2,1)}), bf16[2048,256]{1,0:T(8,128)(2,1)}) %all-gather.38.cloned.1.call-update) | async-done | bytes 1048592 | tf_op jit(solution)/shard_map/all_gather | solution.py:97
  122.2 20.3 %all-gather.40.cloned.1.call-done = bf16[2048,256]{0,1:T(8,128)(2,1)} async-done(((bf16[256,256]{0,1:T(8,128)(2,1)}), bf16[2048,256]{0,1:T(8,128)(2,1)}) %all-gather.40.cloned.1.call-update) | async-done | bytes 1048592 | tf_op jit(solution)/shard_map/all_gather | solution.py:96
  150.4 22.0 %all-gather.26.cloned.1.call-done = bf16[512,2048]{1,0:T(8,128)(2,1)} async-done(((bf16[512,256]{1,0:T(8,128)(2,1)}), bf16[512,2048]{1,0:T(8,128)(2,1)}) %all-gather.26.cloned.1.call-update) | async-done | bytes 2097168 | tf_op jit(solution)/shard_map/all_gather | solution.py:250
  175.8 52.0 %all-reduce.25.cloned.1.call-done = bf16[256,2048]{1,0:T(8,128)(2,1)} async-done(((bf16[256,2048]{1,0:T(8,128)(2,1)}), bf16[256,2048]{1,0:T(8,128)(2,1)}) %all-reduce.25.cloned.1.call-update) | async-done | bytes 1048592 | tf_op jit(solution)/shard_map/psum | solution.py:110
  262.1 20.4 %all-gather.18.cloned.1.call-done = bf16[2048,256]{1,0:T(8,128)(2,1)} async-done(((bf16[256,256]{1,0:T(8,128)(2,1)}), bf16[2048,256]{1,0:T(8,128)(2,1)}) %all-gather.18.cloned.1.call-update) | async-done | bytes 1048592 | tf_op jit(solution)/shard_map/all_gather | solution.py:97
  284.6 23.5 %all-gather.34.cloned.1.call-done = bf16[2048,256]{1,0:T(8,128)(2,1)} async-done(((bf16[256,256]{1,0:T(8,128)(2,1)}), bf16[2048,256]{1,0:T(8,128)(2,1)}) %all-gather.34.cloned.1.call-update) | async-done | bytes 1048592 | tf_op jit(solution)/shard_map/all_gather | solution.py:97
  310.5 23.6 %all-gather.44.cloned.1.call-done = bf16[2048,256]{0,1:T(8,128)(2,1)} async-done(((bf16[256,256]{0,1:T(8,128)(2,1)}), bf16[2048,256]{0,1:T(8,128)(2,1)}) %all-gather.44.cloned.1.call-update) | async-done | bytes 1048592 | tf_op jit(solution)/shard_map/all_gather | solution.py:96
  344.3 15.1 all-gather.22.cloned.1.call-done
  369.8 15.0 all-gather.36.cloned.1.call-done
  395.0 36.9 %all-gather.28.cloned.1.call-done = bf16[2048,1536]{1,0:T(8,128)(2,1)} async-done(((bf16[256,1536]{1,0:T(8,128)(2,1)}), bf16[2048,1536]{1,0:T(8,128)(2,1)}) %all-gather.28.cloned.1.call-update) | async-done | bytes 6291472 | tf_op jit(solution)/shard_map/all_gather | solution.py:251
  437.6 42.6 %all-gather.32.cloned.1.call-done = bf16[1536,2048]{1,0:T(8,128)(2,1)} async-done(((bf16[1536,256]{1,0:T(8,128)(2,1)}), bf16[1536,2048]{1,0:T(8,128)(2,1)}) %all-gather.32.cloned.1.call-update) | async-done | bytes 6291472 | tf_op jit(solution)/shard_map/all_gather | solution.py:253
  486.3 41.1 %all-gather.30.cloned.1.call-done = bf16[2048,1536]{1,0:T(8,128)(2,1)} async-done(((bf16[256,1536]{1,0:T(8,128)(2,1)}), bf16[2048,1536]{1,0:T(8,128)(2,1)}) %all-gather.30.cloned.1.call-update) | async-done | bytes 6291472 | tf_op jit(solution)/shard_map/all_gather | solution.py:252
  527.4 6.8 multiply_convert_fusion.9
  543.0 155.1 %all-reduce.31.cloned.1.call-done = (bf16[256,2048]{1,0:T(8,128)(2,1)}, bf16[256,2048]{1,0:T(8,128)(2,1)}, bf16[256,2048]{1,0:T(8,128)(2,1)}, bf16[256,2048]{1,0:T(8,128)(2,1)}) async-done(((bf16[256,2048]{1,0:T(8,128)(2,1)}, bf16[256,2048]{1,0:T(8,128)(2,1)}, bf16[256,2048]{1,0:T(8,128)(2,1)}, bf16[256,2048]{1,0:T(8,128)(2,1)}), (bf16[256,2048]{1,0:T(8,128)(2,1)}, bf16[256,2048]{1,0:T(8,128)(2,1)}, ...) | async-done | bytes 4194320 | tf_op jit(solution)/shard_map/psum | solution.py:110
  706.5 6.9 fusion.382
  770.9 119.5 %all-reduce.29.cloned.1.call-done = (bf16[256,2048]{1,0:T(8,128)(2,1)}, bf16[256,2048]{1,0:T(8,128)(2,1)}, bf16[256,2048]{1,0:T(8,128)(2,1)}) async-done(((bf16[256,2048]{1,0:T(8,128)(2,1)}, bf16[256,2048]{1,0:T(8,128)(2,1)}, bf16[256,2048]{1,0:T(8,128)(2,1)}), (bf16[256,2048]{1,0:T(8,128)(2,1)}, bf16[256,2048]{1,0:T(8,128)(2,1)}, bf16[256,2048]{1,0:T(8,128)(2,1)})) %all-reduce.29.cloned.1.call-update) | async-done | bytes 3145744 | tf_op jit(solution)/shard_map/psum | solution.py:137
  890.4 7.6 multiply_reduce_fusion
  925.0 6.6 fusion.9
  932.6 6.7 fusion.11
  942.0 6.6 fusion
  949.6 6.8 fusion.2
  1026.8 7.6 fusion.398
  1034.4 6.5 fusion.396
  1058.6 15.3 reduce-scatter.20.cloned.1.call-done
  1084.1 7.5 fusion.397
  1091.6 22.0 %reduce-scatter.18.cloned.1.call-done = bf16[256,256]{0,1:T(8,128)(2,1)} async-done(((bf16[2048,256]{0,1:T(8,128)(2,1)}), bf16[256,256]{0,1:T(8,128)(2,1)}) %reduce-scatter.18.cloned.1.call-update) | async-done | bytes 131088 | tf_op jit(solution)/shard_map/reduce_scatter | solution.py:168
  1116.7 35.9 %reduce-scatter.22.cloned.1.call-done = bf16[256,256]{0,1:T(8,128)(2,1)} async-done(((bf16[2048,256]{0,1:T(8,128)(2,1)}), bf16[256,256]{0,1:T(8,128)(2,1)}) %reduce-scatter.22.cloned.1.call-update) | async-done | bytes 131088 | tf_op jit(solution)/shard_map/reduce_scatter | solution.py:168
  1156.5 35.3 %reduce-scatter.26.cloned.1.call-done = bf16[256,256]{0,1:T(8,128)(2,1)} async-done(((bf16[2048,256]{0,1:T(8,128)(2,1)}), bf16[256,256]{0,1:T(8,128)(2,1)}) %reduce-scatter.26.cloned.1.call-update) | async-done | bytes 131088 | tf_op jit(solution)/shard_map/reduce_scatter | solution.py:168
  1195.7 35.7 %reduce-scatter.30.cloned.1.call-done = bf16[256,256]{0,1:T(8,128)(2,1)} async-done(((bf16[2048,256]{0,1:T(8,128)(2,1)}), bf16[256,256]{0,1:T(8,128)(2,1)}) %reduce-scatter.30.cloned.1.call-update) | async-done | bytes 131088 | tf_op jit(solution)/shard_map/reduce_scatter | solution.py:168
  1235.1 18.2 add_convert_fusion.2
  1253.5 8.0 fusion.401
  1261.5 6.5 fusion.399
  1268.0 6.4 fusion.400
  1274.4 17.4 add_convert_fusion.1
  1292.9 7.8 fusion.177
  1300.7 6.5 fusion.185
  1307.2 6.3 fusion.181
  1313.5 17.3 add_convert_fusion
  1372.4 27.0 %reduce-scatter.36.cloned.1.call-done = bf16[256,256]{1,0:T(8,128)(2,1)} async-done(((bf16[2048,256]{1,0:T(8,128)(2,1)}), bf16[256,256]{1,0:T(8,128)(2,1)}) %reduce-scatter.36.cloned.1.call-update) | async-done | bytes 131088 | tf_op jit(solution)/shard_map/reduce_scatter | solution.py:269
  1401.1 64.1 %reduce-scatter.40.cloned.1.call-done = bf16[256,1536]{1,0:T(8,128)(2,1)} async-done(((bf16[2048,1536]{1,0:T(8,128)(2,1)}), bf16[256,1536]{1,0:T(8,128)(2,1)}) %reduce-scatter.40.cloned.1.call-update) | async-done | bytes 786448 | tf_op jit(solution)/shard_map/reduce_scatter | solution.py:275
  1467.7 62.7 %reduce-scatter.42.cloned.1.call-done = bf16[256,1536]{1,0:T(8,128)(2,1)} async-done(((bf16[2048,1536]{1,0:T(8,128)(2,1)}), bf16[256,1536]{1,0:T(8,128)(2,1)}) %reduce-scatter.42.cloned.1.call-update) | async-done | bytes 786448 | tf_op jit(solution)/shard_map/reduce_scatter | solution.py:278
  1532.9 62.4 %reduce-scatter.44.cloned.1.call-done = bf16[1536,256]{1,0:T(8,128)(2,1)} async-done(((bf16[1536,2048]{1,0:T(8,128)(2,1)}), bf16[1536,256]{1,0:T(8,128)(2,1)}) %reduce-scatter.44.cloned.1.call-update) | async-done | bytes 786448 | tf_op jit(solution)/shard_map/reduce_scatter | solution.py:281
  1597.7 292.1 %all-reduce.27.cloned.1.call-done = (bf16[256,2048]{1,0:T(8,128)(2,1)}, bf16[256,2048]{1,0:T(8,128)(2,1)}, bf16[256,2048]{1,0:T(8,128)(2,1)}, bf16[256,2048]{1,0...) async-done(((bf16[256,2048]{1,0:T(8,128)(2,1)}, bf16[256,2048]{1,0:T(8,128)(2,1)}, ...) | async-done | bytes 8388624 | tf_op jit(solution)/shard_map/psum | solution.py:122
  1889.9 6.5 fusion.111
  1913.2 39.5 %all-reduce.16 = (f32[2048]{0:T(1024)}, f32[2048]{0:T(1024)}, f32[128]{0:T(128)}, f32[128]{0:T(128)}) all-reduce(f32[2048]{0:T(1024)S(1)} %add_add_fusion.17, f32[2048]{0:T(1024)S(1)} %add_add_fusion.16, f32[128]{0:T(128)S(1)} %add_add_fusion.19, f32[128]{0:T(128)S(1)} %add_add_fusion.18), channel_id=1, replica_groups=mesh['wide'=8,'narrow'=4] {'wide','narrow'}, use_global_device_ids=true, to_apply=%region_91.92 | all-reduce | flops 4352 | bytes 34816 | tf_op jit(solution)/shard_map/psum | solution.py:285
  (850 shorter events, 407.8 us)
Async XLA Ops:
  7.2 28.8 %all-gather.16.cloned.1.call-start = ((), (), s32[]{:S(2)}) async-start(), calls=%async_computation.15 | async-start | bytes 1179648 | tf_op jit(solution)/shard_map/all_gather | solution.py:249
  7.9 53.4 %all-gather.20.cloned.1.call-start = ((), (), s32[]{:S(2)}) async-start(), calls=%async_computation.17 | async-start | bytes 1179648 | tf_op jit(solution)/shard_map/all_gather | solution.py:248
  8.7 82.3 %all-gather.24.cloned.1.call-start = ((), (), s32[]{:S(2)}) async-start(), calls=%async_computation.19 | async-start | bytes 2359296 | tf_op jit(solution)/shard_map/all_gather | solution.py:247
  9.4 107.3 %all-gather.38.cloned.1.call-start = ((), (), s32[]{:S(2)}) async-start(), calls=%async_computation.26 | async-start | bytes 1179648 | tf_op jit(solution)/shard_map/all_gather | solution.py:97
  14.1 24.8 %copy-start.229 = (f32[256]{0:T(256)}, f32[256]{0:T(256)S(1)}, u32[]{:S(2)}) copy-start(f32[256]{0:T(256)S(1)} %fusion.118) | copy-start | bytes 3076
  14.1 103.9 %copy-start.194 = (f32[256]{0:T(256)}, f32[256]{0:T(256)S(1)}, u32[]{:S(2)}) copy-start(f32[256]{0:T(256)S(1)} %fusion.321) | copy-start | bytes 3076
  38.7 103.8 %all-gather.40.cloned.1.call-start = ((), (), s32[]{:S(2)}) async-start(), calls=%async_computation.27 | async-start | bytes 1179648 | tf_op jit(solution)/shard_map/all_gather | solution.py:96
  39.5 81.9 %copy-start.56 = (f32[256,128]{0,1:T(8,128)}, f32[256,128]{0,1:T(8,128)S(1)}, u32[]{:S(2)}) copy-start(f32[256,128]{0,1:T(8,128)S(1)} %get-tuple-element.143) | copy-start | bytes 393220
  39.5 81.9 %copy-start.96 = (f32[256,128]{0,1:T(8,128)}, f32[256,128]{0,1:T(8,128)S(1)}, u32[]{:S(2)}) copy-start(f32[256,128]{0,1:T(8,128)S(1)} %get-tuple-element.144) | copy-start | bytes 393220
  66.5 105.9 %all-gather.26.cloned.1.call-start = ((), (), s32[]{:S(2)}) async-start(), calls=%async_computation.20 | async-start | bytes 2359296 | tf_op jit(solution)/shard_map/all_gather | solution.py:250
  67.1 160.7 %all-reduce.25.cloned.1.call-start = ((), (), s32[]{:S(2)}) async-start(), calls=%async_computation.28 | async-start | bytes 2097152 | tf_op jit(solution)/shard_map/psum | solution.py:110
  118.1 28.4 %copy-start.81 = (bf16[2048,2,128]{2,1,0:T(2,128)(2,1)}, bf16[2048,2,128]{2,1,0:T(2,128)(2,1)S(1)}, u32[]{:S(2)}) copy-start(bf16[2048,2,128]{2,1,0:T(2,128)(2,1)S(1)} %reshape.1307) | copy-start | bytes 3145732
  150.3 25.3 %copy-start.156 = (bf16[2,128,2,256]{3,1,2,0:T(8,128)(2,1)}, bf16[2,128,2,256]{3,1,2,0:T(8,128)(2,1)S(1)}, u32[]{:S(2)}) copy-start(bf16[2,128,2,256]{3,1,2,0:T(8,128)(2,1)S(1)} %fusion.167) | copy-start | bytes 786436
  175.7 55.6 %copy-start.40 = (bf16[2048,256]{1,0:T(8,128)(2,1)S(1)}, bf16[2048,256]{1,0:T(8,128)(2,1)}, u32[]{:S(2)}) copy-start(bf16[2048,256]{1,0:T(8,128)(2,1)} %all-gather.16.cloned.1.call-done) | copy-start | bytes 3145732
  175.7 83.8 %all-gather.42.cloned.1.call-start = ((), (), s32[]{:S(2)}) async-start(), calls=%async_computation.29 | async-start | bytes 1179648 | tf_op jit(solution)/shard_map/all_gather | solution.py:97
  233.7 48.7 %all-gather.18.cloned.1.call-start = ((), (), s32[]{:S(2)}) async-start(), calls=%async_computation.16 | async-start | bytes 1179648 | tf_op jit(solution)/shard_map/all_gather | solution.py:97
  236.4 71.8 %all-gather.34.cloned.1.call-start = ((), (), s32[]{:S(2)}) async-start(), calls=%async_computation.24 | async-start | bytes 1179648 | tf_op jit(solution)/shard_map/all_gather | solution.py:97
  241.7 92.4 %all-gather.44.cloned.1.call-start = ((), (), s32[]{:S(2)}) async-start(), calls=%async_computation.30 | async-start | bytes 1179648 | tf_op jit(solution)/shard_map/all_gather | solution.py:96
  246.5 112.8 %all-gather.22.cloned.1.call-start = ((), (), s32[]{:S(2)}) async-start(), calls=%async_computation.18 | async-start | bytes 1179648 | tf_op jit(solution)/shard_map/all_gather | solution.py:96
  247.9 136.9 %all-gather.36.cloned.1.call-start = ((), (), s32[]{:S(2)}) async-start(), calls=%async_computation.25 | async-start | bytes 1179648 | tf_op jit(solution)/shard_map/all_gather | solution.py:96
  249.2 182.8 %all-gather.28.cloned.1.call-start = ((), (), s32[]{:S(2)}) async-start(), calls=%async_computation.21 | async-start | bytes 7077888 | tf_op jit(solution)/shard_map/all_gather | solution.py:251
  249.7 230.5 %all-gather.32.cloned.1.call-start = ((), (), s32[]{:S(2)}) async-start(), calls=%async_computation.23 | async-start | bytes 7077888 | tf_op jit(solution)/shard_map/all_gather | solution.py:253
  250.3 277.1 %all-gather.30.cloned.1.call-start = ((), (), s32[]{:S(2)}) async-start(), calls=%async_computation.22 | async-start | bytes 7077888 | tf_op jit(solution)/shard_map/all_gather | solution.py:252
  250.9 447.3 %all-reduce.31.cloned.1.call-start = ((), (), s32[]{:S(2)}) async-start(), calls=%async_computation.48 | async-start | bytes 8388608 | tf_op jit(solution)/shard_map/psum | solution.py:110
  257.7 76.5 %copy-start.136 = (bf16[256,4,128]{0,2,1:T(8,128)(2,1)}, bf16[256,4,128]{0,2,1:T(8,128)(2,1)S(1)}, u32[]{:S(2)}) copy-start(bf16[256,4,128]{0,2,1:T(8,128)(2,1)S(1)} %fusion.248) | copy-start | bytes 786436
  259.0 125.8 %copy-start.134 = (bf16[256,4,128]{0,2,1:T(8,128)(2,1)}, bf16[256,4,128]{0,2,1:T(8,128)(2,1)S(1)}, u32[]{:S(2)}) copy-start(bf16[256,4,128]{0,2,1:T(8,128)(2,1)S(1)} %fusion.244) | copy-start | bytes 786436
  259.5 267.9 %copy-start.50 = (bf16[256,2048]{1,0:T(8,128)(2,1)}, bf16[256,2048]{1,0:T(8,128)(2,1)S(1)}, u32[]{:S(2)}) copy-start(bf16[256,2048]{1,0:T(8,128)(2,1)S(1)} %multiply_convert_fusion.1) | copy-start | bytes 3145732
  543.0 347.4 %all-reduce.29.cloned.1.call-start = ((), (), s32[]{:S(2)}) async-start(), calls=%async_computation.47 | async-start | bytes 6291456 | tf_op jit(solution)/shard_map/psum | solution.py:137
  733.0 26.6 %copy-start.110 = (bf16[256,1536]{1,0:T(8,128)(2,1)}, bf16[256,1536]{1,0:T(8,128)(2,1)S(1)}, u32[]{:S(2)}) copy-start(bf16[256,1536]{1,0:T(8,128)(2,1)S(1)} %get-tuple-element.99) | copy-start | bytes 2359300
  770.1 278.1 %reduce-scatter.24.cloned.1.call-start = ((), (), s32[]{:S(2)}) async-start(), calls=%async_computation.35 | async-start | bytes 1179648 | tf_op jit(solution)/shard_map/reduce_scatter | solution.py:162
  770.8 144.9 %copy-start.190 = (f32[2,2,256]{2,1,0:T(2,128)}, f32[2,2,256]{2,1,0:T(2,128)S(1)}, u32[]{:S(2)}) copy-start(f32[2,2,256]{2,1,0:T(2,128)S(1)} %log_add_fusion.1) | copy-start | bytes 12292
  770.8 178.7 %copy-start.188 = (f32[2,2,256]{2,1,0:T(2,128)}, f32[2,2,256]{2,1,0:T(2,128)S(1)}, u32[]{:S(2)}) copy-start(f32[2,2,256]{2,1,0:T(2,128)S(1)} %log_add_fusion) | copy-start | bytes 12292
  920.7 129.1 %reduce-scatter.16.cloned.1.call-start = ((), (), s32[]{:S(2)}) async-start(), calls=%async_computation.31 | async-start | bytes 1179648 | tf_op jit(solution)/shard_map/reduce_scatter | solution.py:162
  941.9 109.7 %reduce-scatter.28.cloned.1.call-start = ((), (), s32[]{:S(2)}) async-start(), calls=%async_computation.37 | async-start | bytes 1179648 | tf_op jit(solution)/shard_map/reduce_scatter | solution.py:162
  958.9 114.9 %reduce-scatter.20.cloned.1.call-start = ((), (), s32[]{:S(2)}) async-start(), calls=%async_computation.33 | async-start | bytes 1179648 | tf_op jit(solution)/shard_map/reduce_scatter | solution.py:162
  969.1 144.5 %reduce-scatter.18.cloned.1.call-start = ((), (), s32[]{:S(2)}) async-start(), calls=%async_computation.32 | async-start | bytes 1179648 | tf_op jit(solution)/shard_map/reduce_scatter | solution.py:168
  980.4 172.2 %reduce-scatter.22.cloned.1.call-start = ((), (), s32[]{:S(2)}) async-start(), calls=%async_computation.34 | async-start | bytes 1179648 | tf_op jit(solution)/shard_map/reduce_scatter | solution.py:168
  991.2 200.6 %reduce-scatter.26.cloned.1.call-start = ((), (), s32[]{:S(2)}) async-start(), calls=%async_computation.36 | async-start | bytes 1179648 | tf_op jit(solution)/shard_map/reduce_scatter | solution.py:168
  1003.1 228.3 %reduce-scatter.30.cloned.1.call-start = ((), (), s32[]{:S(2)}) async-start(), calls=%async_computation.38 | async-start | bytes 1179648 | tf_op jit(solution)/shard_map/reduce_scatter | solution.py:168
  1017.1 349.9 %reduce-scatter.32.cloned.1.call-start = ((), (), s32[]{:S(2)}) async-start(), calls=%async_computation.39 | async-start | bytes 2359296 | tf_op jit(solution)/shard_map/reduce_scatter | solution.py:263
  1025.6 343.1 %reduce-scatter.38.cloned.1.call-start = ((), (), s32[]{:S(2)}) async-start(), calls=%async_computation.42 | async-start | bytes 2359296 | tf_op jit(solution)/shard_map/reduce_scatter | solution.py:272
  1048.1 322.7 %reduce-scatter.34.cloned.1.call-start = ((), (), s32[]{:S(2)}) async-start(), calls=%async_computation.40 | async-start | bytes 1179648 | tf_op jit(solution)/shard_map/reduce_scatter | solution.py:266
  1083.6 315.9 %reduce-scatter.36.cloned.1.call-start = ((), (), s32[]{:S(2)}) async-start(), calls=%async_computation.41 | async-start | bytes 1179648 | tf_op jit(solution)/shard_map/reduce_scatter | solution.py:269
  1235.0 230.2 %reduce-scatter.40.cloned.1.call-start = ((), (), s32[]{:S(2)}) async-start(), calls=%async_computation.43 | async-start | bytes 7077888 | tf_op jit(solution)/shard_map/reduce_scatter | solution.py:275
  1253.3 277.1 %reduce-scatter.42.cloned.1.call-start = ((), (), s32[]{:S(2)}) async-start(), calls=%async_computation.44 | async-start | bytes 7077888 | tf_op jit(solution)/shard_map/reduce_scatter | solution.py:278
  1291.8 303.5 %reduce-scatter.44.cloned.1.call-start = ((), (), s32[]{:S(2)}) async-start(), calls=%async_computation.45 | async-start | bytes 7077888 | tf_op jit(solution)/shard_map/reduce_scatter | solution.py:281
  1330.8 559.0 %all-reduce.27.cloned.1.call-start = ((), (), s32[]{:S(2)}) async-start(), calls=%async_computation.46 | async-start | bytes 16777216 | tf_op jit(solution)/shard_map/psum | solution.py:122
  1467.7 422.1 %copy-start.202 = (f32[256]{0:T(256)S(1)}, f32[256]{0:T(256)}, u32[]{:S(2)}) copy-start(f32[256]{0:T(256)} %copy-done.199) | copy-start | bytes 3076
  (251 other events, 1176.5 us)
Sparse Core Ops, SparseCore 0:
  9.9 26.0 all-gather.15
  37.9 23.3 all-gather.19
  63.2 27.7 all-gather.23
  93.3 23.3 all-gather.37
  119.0 23.4 all-gather.39
  144.3 28.0 all-gather.25
  175.8 51.8 all-reduce.24
  233.9 22.6 all-gather.41
  259.0 23.3 all-gather.17
  284.8 23.3 all-gather.33
  310.6 23.4 all-gather.43
  335.9 23.4 all-gather.21
  361.2 23.4 all-gather.35
  386.5 45.3 all-gather.27
  433.6 46.5 all-gather.31
  482.0 45.3 all-gather.29
  543.1 155.0 all-reduce.30
  770.3 120.0 all-reduce.28
  920.9 34.9 reduce-scatter.23
  959.5 35.9 reduce-scatter.15
  998.7 35.9 reduce-scatter.27
  1037.8 35.9 reduce-scatter.19
  1077.6 35.9 reduce-scatter.17
  1116.6 35.9 reduce-scatter.21
  1155.8 35.9 reduce-scatter.25
  1195.4 35.9 reduce-scatter.29
  1234.5 41.1 reduce-scatter.31
  1279.0 41.1 reduce-scatter.37
  1323.9 35.9 reduce-scatter.33
  1363.5 35.9 reduce-scatter.35
  1403.4 61.7 reduce-scatter.39
  1468.6 61.7 reduce-scatter.41
  1533.7 61.5 reduce-scatter.43
  1598.7 291.0 all-reduce.26
where the time goes:
time: 1970 us; the launch traced here: 1960 us
  waiting for transfers between devices  1330 us (68%)
  matrix products  388 us (20%)
  other arithmetic  128 us (6%)
  local copies, waits for them, and re-layouts  54.3 us (3%)
  blocking collectives  39.5 us (2%)
    psum x1, waiting for transfers between devices, one_batch(): lax.psum(ffn_part.astype(jnp.bfloat16), 'narrow').astype(jnp.float32)  292 us
    psum x2, waiting for transfers between devices, one_batch(): lax.psum(attn_part.astype(jnp.bfloat16), 'narrow').astype(jnp.float32)  207 us
    reduce_scatter x4, waiting for transfers between devices, one_batch(): lax.psum_scatter(grad_valueall.reshape(total, groups * HD).astype(jnp.bfl...  129 us
    psum x1, waiting for transfers between devices, one_batch(): lax.psum(partial_two.astype(jnp.bfloat16), 'narrow').astype(jnp.float32)  119 us
    all_gather x4, waiting for transfers between devices, one_batch(): lax.all_gather(key_low, 'wide', axis=0, tiled=True)  74 us
    all_gather x4, waiting for transfers between devices, one_batch(): lax.all_gather(value_low, 'wide', axis=0, tiled=True)  65.8 us
    reduce_scatter x1, waiting for transfers between devices, local(): lax.psum_scatter(totals[4].astype(jnp.bfloat16), 'wide', scatter_dimensio...  64.1 us
    reduce_scatter x1, waiting for transfers between devices, local(): lax.psum_scatter(totals[5].astype(jnp.bfloat16), 'wide', scatter_dimensio...  62.7 us
  transfers between devices with their start and end apart: 34, of which 28 were waited for; matrix products, arithmetic and copies ran while one was open for 20% of the time, Pallas kernels for 0%

commit v1 on v0

--- a/solution.py
+++ b/solution.py
@@ -134,7 +134,11 @@
     gain_two = jnp.sum(partial_two * unit_two, axis=0)
     grad_middle = (
         grad_float
-        + pull_two(lax.psum(partial_two.astype(jnp.bfloat16), "narrow").astype(jnp.float32))[0]
+        + pull_two(
+            lax.all_gather(partial_two.astype(jnp.bfloat16), "narrow")
+            .sum(axis=0)
+            .astype(jnp.float32)
+        )[0]
     )
     middle_low = grad_middle.astype(jnp.bfloat16)
     grad_wout = jnp.einsum("th,td->hd", mixed_low, middle_low, preferred_element_type=jnp.float32)

time: 1970 us -> 2080 us (1.056)
  waiting for transfers between devices: 1330 us -> 1430 us
  other arithmetic: 128 us -> 150 us
    all_gather x0 -> x4, waiting for transfers between devices: none -> 263 us  [one_batch(): lax.all_gather(partial_two.astype(jnp.bfloat16), 'narrow').sum(axis=0)]
    psum x1 -> x0, waiting for transfers between devices: 119 us -> none  [one_batch(): lax.psum(partial_two.astype(jnp.bfloat16), 'narrow').astype(jnp.float32)]
    all_gather x4, waiting for transfers between devices: 74 us -> 36.7 us  [one_batch(): lax.all_gather(key_low, 'wide', axis=0, tiled=True)]
    psum x2, waiting for transfers between devices: 207 us -> 170 us  [one_batch(): lax.psum(attn_part.astype(jnp.bfloat16), 'narrow').astype(jnp.float32)]
    reduce_scatter x1, waiting for transfers between devices: 27 us -> 0.01 us  [local(): lax.psum_scatter(totals[2].astype(jnp.bfloat16), 'wide', scatter_dimensio...]
    reduce_scatter x4, waiting for transfers between devices: 15.3 us -> 36.9 us  [one_batch(): lax.psum_scatter(grad_keyall.reshape(total, groups * HD).astype(jnp.bfloa...]
  transfers between devices with their start and end apart: 34 -> 37, of which waited for: 28 -> 30; matrix products, arithmetic and copies ran while one was open for 20% -> 22% of each run, Pallas kernels for 0% -> 0%
where the time goes in v1:
time: 2080 us; the launch traced here: 2070 us
  waiting for transfers between devices  1430 us (69%)
  matrix products  382 us (18%)
  other arithmetic  150 us (7%)
  local copies, waits for them, and re-layouts  51.4 us (2%)
  blocking collectives  39.5 us (2%)
    psum x1, waiting for transfers between devices, one_batch(): lax.psum(ffn_part.astype(jnp.bfloat16), 'narrow').astype(jnp.float32)  292 us
    all_gather x4, waiting for transfers between devices, one_batch(): lax.all_gather(partial_two.astype(jnp.bfloat16), 'narrow').sum(axis=0)  263 us
    psum x2, waiting for transfers between devices, one_batch(): lax.psum(attn_part.astype(jnp.bfloat16), 'narrow').astype(jnp.float32)  170 us
    reduce_scatter x4, waiting for transfers between devices, one_batch(): lax.psum_scatter(grad_valueall.reshape(total, groups * HD).astype(jnp.bfl...  142 us
    all_gather x4, waiting for transfers between devices, one_batch(): lax.all_gather(value_low, 'wide', axis=0, tiled=True)  81.5 us
    reduce_scatter x1, waiting for transfers between devices, local(): lax.psum_scatter(totals[5].astype(jnp.bfloat16), 'wide', scatter_dimensio...  62.7 us
    reduce_scatter x1, waiting for transfers between devices, local(): lax.psum_scatter(totals[6].astype(jnp.bfloat16), 'wide', scatter_dimensio...  62.4 us
    reduce_scatter x1, waiting for transfers between devices, local(): lax.psum_scatter(totals[4].astype(jnp.bfloat16), 'wide', scatter_dimensio...  62.4 us
  transfers between devices with their start and end apart: 37, of which 30 were waited for; matrix products, arithmetic and copies ran while one was open for 22% of the time, Pallas kernels for 0%

profile of v1, /device:TPU:0, one launch (start us, length us, event | category | flops | bytes accessed | tf_op | source)
XLA Modules:
  0.0 2072.7 jit_solution(1971729719539140949)
XLA Ops:
  14.1 21.9 %all-gather.24.cloned.1.call-done = bf16[2048,256]{1,0:T(8,128)(2,1)} async-done(((bf16[256,256]{1,0:T(8,128)(2,1)}), bf16[2048,256]{1,0:T(8,128)(2,1)}) %all-gather.24.cloned.1.call-update) | async-done | bytes 1048592 | tf_op jit(solution)/shard_map/all_gather | solution.py:253
  40.2 21.1 %all-gather.28.cloned.1.call-done = bf16[2048,256]{1,0:T(8,128)(2,1)} async-done(((bf16[256,256]{1,0:T(8,128)(2,1)}), bf16[2048,256]{1,0:T(8,128)(2,1)}) %all-gather.28.cloned.1.call-update) | async-done | bytes 1048592 | tf_op jit(solution)/shard_map/all_gather | solution.py:252
  71.8 19.2 all-gather.32.cloned.1.call-done
  94.9 21.8 %all-gather.46.cloned.1.call-done = bf16[2048,256]{1,0:T(8,128)(2,1)} async-done(((bf16[256,256]{1,0:T(8,128)(2,1)}), bf16[2048,256]{1,0:T(8,128)(2,1)}) %all-gather.46.cloned.1.call-update) | async-done | bytes 1048592 | tf_op jit(solution)/shard_map/all_gather | solution.py:97
  122.2 20.3 all-gather.48.cloned.1.call-done
  150.3 22.1 %all-gather.34.cloned.1.call-done = bf16[512,2048]{1,0:T(8,128)(2,1)} async-done(((bf16[512,256]{1,0:T(8,128)(2,1)}), bf16[512,2048]{1,0:T(8,128)(2,1)}) %all-gather.34.cloned.1.call-update) | async-done | bytes 2097168 | tf_op jit(solution)/shard_map/all_gather | solution.py:254
  176.5 51.3 %all-reduce.23.cloned.1.call-done = bf16[256,2048]{1,0:T(8,128)(2,1)} async-done(((bf16[256,2048]{1,0:T(8,128)(2,1)}), bf16[256,2048]{1,0:T(8,128)(2,1)}) %all-reduce.23.cloned.1.call-update) | async-done | bytes 1048592 | tf_op jit(solution)/shard_map/psum | solution.py:110
  269.8 13.6 all-gather.50.cloned.1.call-done
  285.5 23.0 %all-gather.26.cloned.1.call-done = bf16[2048,256]{1,0:T(8,128)(2,1)} async-done(((bf16[256,256]{1,0:T(8,128)(2,1)}), bf16[2048,256]{1,0:T(8,128)(2,1)}) %all-gather.26.cloned.1.call-update) | async-done | bytes 1048592 | tf_op jit(solution)/shard_map/all_gather | solution.py:97
  310.7 23.1 %all-gather.42.cloned.1.call-done = bf16[2048,256]{1,0:T(8,128)(2,1)} async-done(((bf16[256,256]{1,0:T(8,128)(2,1)}), bf16[2048,256]{1,0:T(8,128)(2,1)}) %all-gather.42.cloned.1.call-update) | async-done | bytes 1048592 | tf_op jit(solution)/shard_map/all_gather | solution.py:97
  335.9 45.0 %all-gather.36.cloned.1.call-done = bf16[2048,1536]{1,0:T(8,128)(2,1)} async-done(((bf16[256,1536]{1,0:T(8,128)(2,1)}), bf16[2048,1536]{1,0:T(8,128)(2,1)}) %all-gather.36.cloned.1.call-update) | async-done | bytes 6291472 | tf_op jit(solution)/shard_map/all_gather | solution.py:255
  386.7 42.8 %all-gather.40.cloned.1.call-done = bf16[1536,2048]{1,0:T(8,128)(2,1)} async-done(((bf16[1536,256]{1,0:T(8,128)(2,1)}), bf16[1536,2048]{1,0:T(8,128)(2,1)}) %all-gather.40.cloned.1.call-update) | async-done | bytes 6291472 | tf_op jit(solution)/shard_map/all_gather | solution.py:257
  435.5 41.1 %all-gather.38.cloned.1.call-done = bf16[2048,1536]{1,0:T(8,128)(2,1)} async-done(((bf16[256,1536]{1,0:T(8,128)(2,1)}), bf16[2048,1536]{1,0:T(8,128)(2,1)}) %all-gather.38.cloned.1.call-update) | async-done | bytes 6291472 | tf_op jit(solution)/shard_map/all_gather | solution.py:256
  476.6 6.8 multiply_convert_fusion.9
  512.0 15.1 all-gather.44.cloned.1.call-done
  537.6 71.7 %all-gather.58.cloned.1.call-done = bf16[1024,2048]{1,0:T(8,128)(2,1)} async-done(((bf16[256,2048]{1,0:T(8,128)(2,1)}), bf16[1024,2048]{1,0:T(8,128)(2,1)}) %all-gather.58.cloned.1.call-update) | async-done | bytes 4194320 | tf_op jit(solution)/shard_map/all_gather | solution.py:138
  613.6 118.9 %all-reduce.27.cloned.1.call-done = (bf16[256,2048]{1,0:T(8,128)(2,1)}, bf16[256,2048]{1,0:T(8,128)(2,1)}, bf16[256,2048]{1,0:T(8,128)(2,1)}) async-done(((bf16[256,2048]{1,0:T(8,128)(2,1)}, bf16[256,2048]{1,0:T(8,128)(2,1)}, bf16[256,2048]{1,0:T(8,128)(2,1)}), (bf16[256,2048]{1,0:T(8,128)(2,1)}, bf16[256,2048]{1,0:T(8,128)(2,1)}, bf16[256,2048]{1,0:T(8,128)(2,1)})) %all-reduce.27.cloned.1.call-update) | async-done | bytes 3145744 | tf_op jit(solution)/shard_map/psum | solution.py:110
  801.0 38.1 %all-gather.56.cloned.1.call-done = bf16[1024,2048]{1,0:T(8,128)(2,1)} async-done(((bf16[256,2048]{1,0:T(8,128)(2,1)}), bf16[1024,2048]{1,0:T(8,128)(2,1)}) %all-gather.56.cloned.1.call-update) | async-done | bytes 4194320 | tf_op jit(solution)/shard_map/all_gather | solution.py:138
  843.4 76.4 %all-gather.60.cloned.1.call-done = bf16[1024,2048]{1,0:T(8,128)(2,1)} async-done(((bf16[256,2048]{1,0:T(8,128)(2,1)}), bf16[1024,2048]{1,0:T(8,128)(2,1)}) %all-gather.60.cloned.1.call-update) | async-done | bytes 4194320 | tf_op jit(solution)/shard_map/all_gather | solution.py:138
  924.1 76.6 %all-gather.54.cloned.1.call-done = bf16[1024,2048]{1,0:T(8,128)(2,1)} async-done(((bf16[256,2048]{1,0:T(8,128)(2,1)}), bf16[1024,2048]{1,0:T(8,128)(2,1)}) %all-gather.54.cloned.1.call-update) | async-done | bytes 4194320 | tf_op jit(solution)/shard_map/all_gather | solution.py:138
  1004.9 7.1 multiply_reduce_fusion
  1040.1 6.6 fusion.9
  1047.7 6.7 fusion.11
  1057.0 6.5 fusion
  1064.5 6.8 fusion.2
  1151.9 35.4 %reduce-scatter.20.cloned.1.call-done = bf16[256,256]{0,1:T(8,128)(2,1)} async-done(((bf16[2048,256]{0,1:T(8,128)(2,1)}), bf16[256,256]{0,1:T(8,128)(2,1)}) %reduce-scatter.20.cloned.1.call-update) | async-done | bytes 131088 | tf_op jit(solution)/shard_map/reduce_scatter | solution.py:166
  1194.4 32.6 %reduce-scatter.18.cloned.1.call-done = bf16[256,256]{0,1:T(8,128)(2,1)} async-done(((bf16[2048,256]{0,1:T(8,128)(2,1)}), bf16[256,256]{0,1:T(8,128)(2,1)}) %reduce-scatter.18.cloned.1.call-update) | async-done | bytes 131088 | tf_op jit(solution)/shard_map/reduce_scatter | solution.py:172
  1228.8 37.2 %reduce-scatter.22.cloned.1.call-done = bf16[256,256]{0,1:T(8,128)(2,1)} async-done(((bf16[2048,256]{0,1:T(8,128)(2,1)}), bf16[256,256]{0,1:T(8,128)(2,1)}) %reduce-scatter.22.cloned.1.call-update) | async-done | bytes 131088 | tf_op jit(solution)/shard_map/reduce_scatter | solution.py:172
  1269.1 36.0 %reduce-scatter.26.cloned.1.call-done = bf16[256,256]{0,1:T(8,128)(2,1)} async-done(((bf16[2048,256]{0,1:T(8,128)(2,1)}), bf16[256,256]{0,1:T(8,128)(2,1)}) %reduce-scatter.26.cloned.1.call-update) | async-done | bytes 131088 | tf_op jit(solution)/shard_map/reduce_scatter | solution.py:172
  1309.1 35.8 %reduce-scatter.30.cloned.1.call-done = bf16[256,256]{0,1:T(8,128)(2,1)} async-done(((bf16[2048,256]{0,1:T(8,128)(2,1)}), bf16[256,256]{0,1:T(8,128)(2,1)}) %reduce-scatter.30.cloned.1.call-update) | async-done | bytes 131088 | tf_op jit(solution)/shard_map/reduce_scatter | solution.py:172
  1357.5 7.7 fusion.398
  1365.2 6.5 fusion.396
  1371.7 6.3 fusion.397
  1378.1 17.4 add_convert_fusion.2
  1395.7 8.0 fusion.401
  1403.7 6.5 fusion.399
  1410.2 6.3 fusion.400
  1416.5 17.2 add_convert_fusion.1
  1434.8 7.8 fusion.177
  1442.6 6.5 fusion.185
  1449.1 6.3 fusion.181
  1455.4 17.3 add_convert_fusion
  1515.8 62.4 %reduce-scatter.40.cloned.1.call-done = bf16[256,1536]{1,0:T(8,128)(2,1)} async-done(((bf16[2048,1536]{1,0:T(8,128)(2,1)}), bf16[256,1536]{1,0:T(8,128)(2,1)}) %reduce-scatter.40.cloned.1.call-update) | async-done | bytes 786448 | tf_op jit(solution)/shard_map/reduce_scatter | solution.py:279
  1580.6 62.7 %reduce-scatter.42.cloned.1.call-done = bf16[256,1536]{1,0:T(8,128)(2,1)} async-done(((bf16[2048,1536]{1,0:T(8,128)(2,1)}), bf16[256,1536]{1,0:T(8,128)(2,1)}) %reduce-scatter.42.cloned.1.call-update) | async-done | bytes 786448 | tf_op jit(solution)/shard_map/reduce_scatter | solution.py:282
  1645.8 62.4 %reduce-scatter.44.cloned.1.call-done = bf16[1536,256]{1,0:T(8,128)(2,1)} async-done(((bf16[1536,2048]{1,0:T(8,128)(2,1)}), bf16[1536,256]{1,0:T(8,128)(2,1)}) %reduce-scatter.44.cloned.1.call-update) | async-done | bytes 786448 | tf_op jit(solution)/shard_map/reduce_scatter | solution.py:285
  1710.5 292.0 %all-reduce.25.cloned.1.call-done = (bf16[256,2048]{1,0:T(8,128)(2,1)}, bf16[256,2048]{1,0:T(8,128)(2,1)}, bf16[256,2048]{1,0:T(8,128)(2,1)}, bf16[256,2048]{1,0...) async-done(((bf16[256,2048]{1,0:T(8,128)(2,1)}, bf16[256,2048]{1,0:T(8,128)(2,1)}, ...) | async-done | bytes 8388624 | tf_op jit(solution)/shard_map/psum | solution.py:122
  2002.6 6.5 fusion.111
  2025.9 39.5 %all-reduce.16 = (f32[2048]{0:T(1024)}, f32[2048]{0:T(1024)}, f32[128]{0:T(128)}, f32[128]{0:T(128)}) all-reduce(f32[2048]{0:T(1024)S(1)} %add_add_fusion.17, f32[2048]{0:T(1024)S(1)} %add_add_fusion.16, f32[128]{0:T(128)S(1)} %add_add_fusion.19, f32[128]{0:T(128)S(1)} %add_add_fusion.18), channel_id=1, replica_groups=mesh['wide'=8,'narrow'=4] {'wide','narrow'}, use_global_device_ids=true, to_apply=%region_91.92 | all-reduce | flops 4352 | bytes 34816 | tf_op jit(solution)/shard_map/psum | solution.py:289
  (903 shorter events, 434.1 us)
Async XLA Ops:
  7.2 28.8 %all-gather.24.cloned.1.call-start = ((), (), s32[]{:S(2)}) async-start(), calls=%async_computation.15 | async-start | bytes 1179648 | tf_op jit(solution)/shard_map/all_gather | solution.py:253
  7.9 53.4 %all-gather.28.cloned.1.call-start = ((), (), s32[]{:S(2)}) async-start(), calls=%async_computation.17 | async-start | bytes 1179648 | tf_op jit(solution)/shard_map/all_gather | solution.py:252
  8.7 82.3 %all-gather.32.cloned.1.call-start = ((), (), s32[]{:S(2)}) async-start(), calls=%async_computation.19 | async-start | bytes 2359296 | tf_op jit(solution)/shard_map/all_gather | solution.py:251
  9.4 107.3 %all-gather.46.cloned.1.call-start = ((), (), s32[]{:S(2)}) async-start(), calls=%async_computation.26 | async-start | bytes 1179648 | tf_op jit(solution)/shard_map/all_gather | solution.py:97
  14.1 103.9 %copy-start.193 = (f32[256]{0:T(256)}, f32[256]{0:T(256)S(1)}, u32[]{:S(2)}) copy-start(f32[256]{0:T(256)S(1)} %fusion.321) | copy-start | bytes 3076
  38.7 103.8 %all-gather.48.cloned.1.call-start = ((), (), s32[]{:S(2)}) async-start(), calls=%async_computation.27 | async-start | bytes 1179648 | tf_op jit(solution)/shard_map/all_gather | solution.py:96
  40.1 81.3 %copy-start.60 = (f32[256,128]{0,1:T(8,128)}, f32[256,128]{0,1:T(8,128)S(1)}, u32[]{:S(2)}) copy-start(f32[256,128]{0,1:T(8,128)S(1)} %get-tuple-element.139) | copy-start | bytes 393220
  40.2 81.3 %copy-start.95 = (f32[256,128]{0,1:T(8,128)}, f32[256,128]{0,1:T(8,128)S(1)}, u32[]{:S(2)}) copy-start(f32[256,128]{0,1:T(8,128)S(1)} %get-tuple-element.140) | copy-start | bytes 393220
  66.5 105.9 %all-gather.34.cloned.1.call-start = ((), (), s32[]{:S(2)}) async-start(), calls=%async_computation.20 | async-start | bytes 2359296 | tf_op jit(solution)/shard_map/all_gather | solution.py:254
  67.1 160.7 %all-reduce.23.cloned.1.call-start = ((), (), s32[]{:S(2)}) async-start(), calls=%async_computation.28 | async-start | bytes 2097152 | tf_op jit(solution)/shard_map/psum | solution.py:110
  175.8 86.3 %all-gather.52.cloned.1.call-start = ((), (), s32[]{:S(2)}) async-start(), calls=%async_computation.30 | async-start | bytes 1179648 | tf_op jit(solution)/shard_map/all_gather | solution.py:96
  176.5 79.8 %copy-start.62 = (f32[256,128]{0,1:T(8,128)}, f32[256,128]{0,1:T(8,128)S(1)}, u32[]{:S(2)}) copy-start(f32[256,128]{0,1:T(8,128)S(1)} %get-tuple-element.137) | copy-start | bytes 393220
  176.5 79.8 %copy-start.97 = (f32[256,128]{0,1:T(8,128)}, f32[256,128]{0,1:T(8,128)S(1)}, u32[]{:S(2)}) copy-start(f32[256,128]{0,1:T(8,128)S(1)} %get-tuple-element.138) | copy-start | bytes 393220
  176.5 55.0 %copy-start.152 = (bf16[256,2048]{1,0:T(8,128)(2,1)S(1)}, bf16[256,2048]{1,0:T(8,128)(2,1)}, u32[]{:S(2)}) copy-start(bf16[256,2048]{1,0:T(8,128)(2,1)} %copy-done.151) | copy-start | bytes 3145732
  235.2 48.2 %all-gather.50.cloned.1.call-start = ((), (), s32[]{:S(2)}) async-start(), calls=%async_computation.29 | async-start | bytes 1179648 | tf_op jit(solution)/shard_map/all_gather | solution.py:97
  237.6 70.9 %all-gather.26.cloned.1.call-start = ((), (), s32[]{:S(2)}) async-start(), calls=%async_computation.16 | async-start | bytes 1179648 | tf_op jit(solution)/shard_map/all_gather | solution.py:97
  240.1 93.7 %all-gather.42.cloned.1.call-start = ((), (), s32[]{:S(2)}) async-start(), calls=%async_computation.24 | async-start | bytes 1179648 | tf_op jit(solution)/shard_map/all_gather | solution.py:97
  242.6 138.4 %all-gather.36.cloned.1.call-start = ((), (), s32[]{:S(2)}) async-start(), calls=%async_computation.21 | async-start | bytes 7077888 | tf_op jit(solution)/shard_map/all_gather | solution.py:255
  243.2 186.3 %all-gather.40.cloned.1.call-start = ((), (), s32[]{:S(2)}) async-start(), calls=%async_computation.23 | async-start | bytes 7077888 | tf_op jit(solution)/shard_map/all_gather | solution.py:257
  243.9 232.7 %all-gather.38.cloned.1.call-start = ((), (), s32[]{:S(2)}) async-start(), calls=%async_computation.22 | async-start | bytes 7077888 | tf_op jit(solution)/shard_map/all_gather | solution.py:256
  244.5 257.4 %all-gather.30.cloned.1.call-start = ((), (), s32[]{:S(2)}) async-start(), calls=%async_computation.18 | async-start | bytes 1179648 | tf_op jit(solution)/shard_map/all_gather | solution.py:96
  253.3 273.8 %all-gather.44.cloned.1.call-start = ((), (), s32[]{:S(2)}) async-start(), calls=%async_computation.25 | async-start | bytes 1179648 | tf_op jit(solution)/shard_map/all_gather | solution.py:96
  253.4 479.1 %copy-start.222 = (f32[256]{0:T(256)}, f32[256]{0:T(256)S(1)}, u32[]{:S(2)}) copy-start(f32[256]{0:T(256)S(1)} %fusion.322) | copy-start | bytes 3076
  257.9 351.4 %all-gather.58.cloned.1.call-start = ((), (), s32[]{:S(2)}) async-start(), calls=%async_computation.48 | async-start | bytes 5242880 | tf_op jit(solution)/shard_map/all_gather | solution.py:138
  262.0 214.6 %copy-start.50 = (bf16[256,2048]{1,0:T(8,128)(2,1)}, bf16[256,2048]{1,0:T(8,128)(2,1)S(1)}, u32[]{:S(2)}) copy-start(bf16[256,2048]{1,0:T(8,128)(2,1)S(1)} %multiply_convert_fusion.1) | copy-start | bytes 3145732
  492.4 240.1 %all-reduce.27.cloned.1.call-start = ((), (), s32[]{:S(2)}) async-start(), calls=%async_computation.51 | async-start | bytes 6291456 | tf_op jit(solution)/shard_map/psum | solution.py:110
  537.2 302.0 %all-gather.56.cloned.1.call-start = ((), (), s32[]{:S(2)}) async-start(), calls=%async_computation.47 | async-start | bytes 5242880 | tf_op jit(solution)/shard_map/all_gather | solution.py:138
  759.3 160.6 %all-gather.60.cloned.1.call-start = ((), (), s32[]{:S(2)}) async-start(), calls=%async_computation.49 | async-start | bytes 5242880 | tf_op jit(solution)/shard_map/all_gather | solution.py:138
  780.4 220.2 %all-gather.54.cloned.1.call-start = ((), (), s32[]{:S(2)}) async-start(), calls=%async_computation.46 | async-start | bytes 5242880 | tf_op jit(solution)/shard_map/all_gather | solution.py:138
  800.6 344.0 %reduce-scatter.24.cloned.1.call-start = ((), (), s32[]{:S(2)}) async-start(), calls=%async_computation.35 | async-start | bytes 1179648 | tf_op jit(solution)/shard_map/reduce_scatter | solution.py:166
  800.9 229.2 %copy-start.189 = (f32[2,2,256]{2,1,0:T(2,128)}, f32[2,2,256]{2,1,0:T(2,128)S(1)}, u32[]{:S(2)}) copy-start(f32[2,2,256]{2,1,0:T(2,128)S(1)} %log_add_fusion.1) | copy-start | bytes 12292
  801.0 263.5 %copy-start.187 = (f32[2,2,256]{2,1,0:T(2,128)}, f32[2,2,256]{2,1,0:T(2,128)S(1)}, u32[]{:S(2)}) copy-start(f32[2,2,256]{2,1,0:T(2,128)S(1)} %log_add_fusion) | copy-start | bytes 12292
  1035.3 110.4 %reduce-scatter.16.cloned.1.call-start = ((), (), s32[]{:S(2)}) async-start(), calls=%async_computation.31 | async-start | bytes 1179648 | tf_op jit(solution)/shard_map/reduce_scatter | solution.py:166
  1056.9 91.2 %reduce-scatter.28.cloned.1.call-start = ((), (), s32[]{:S(2)}) async-start(), calls=%async_computation.37 | async-start | bytes 1179648 | tf_op jit(solution)/shard_map/reduce_scatter | solution.py:166
  1073.8 113.6 %reduce-scatter.20.cloned.1.call-start = ((), (), s32[]{:S(2)}) async-start(), calls=%async_computation.33 | async-start | bytes 1179648 | tf_op jit(solution)/shard_map/reduce_scatter | solution.py:166
  1084.1 142.9 %reduce-scatter.18.cloned.1.call-start = ((), (), s32[]{:S(2)}) async-start(), calls=%async_computation.32 | async-start | bytes 1179648 | tf_op jit(solution)/shard_map/reduce_scatter | solution.py:172
  1096.1 169.9 %reduce-scatter.22.cloned.1.call-start = ((), (), s32[]{:S(2)}) async-start(), calls=%async_computation.34 | async-start | bytes 1179648 | tf_op jit(solution)/shard_map/reduce_scatter | solution.py:172
  1108.8 196.3 %reduce-scatter.26.cloned.1.call-start = ((), (), s32[]{:S(2)}) async-start(), calls=%async_computation.36 | async-start | bytes 1179648 | tf_op jit(solution)/shard_map/reduce_scatter | solution.py:172
  1121.7 223.3 %reduce-scatter.30.cloned.1.call-start = ((), (), s32[]{:S(2)}) async-start(), calls=%async_computation.38 | async-start | bytes 1179648 | tf_op jit(solution)/shard_map/reduce_scatter | solution.py:172
  1135.8 372.9 %reduce-scatter.32.cloned.1.call-start = ((), (), s32[]{:S(2)}) async-start(), calls=%async_computation.39 | async-start | bytes 2359296 | tf_op jit(solution)/shard_map/reduce_scatter | solution.py:267
  1144.5 365.9 %reduce-scatter.34.cloned.1.call-start = ((), (), s32[]{:S(2)}) async-start(), calls=%async_computation.40 | async-start | bytes 1179648 | tf_op jit(solution)/shard_map/reduce_scatter | solution.py:270
  1194.3 317.8 %reduce-scatter.36.cloned.1.call-start = ((), (), s32[]{:S(2)}) async-start(), calls=%async_computation.41 | async-start | bytes 1179648 | tf_op jit(solution)/shard_map/reduce_scatter | solution.py:273
  1348.5 165.5 %reduce-scatter.38.cloned.1.call-start = ((), (), s32[]{:S(2)}) async-start(), calls=%async_computation.42 | async-start | bytes 2359296 | tf_op jit(solution)/shard_map/reduce_scatter | solution.py:276
  1356.2 221.9 %reduce-scatter.40.cloned.1.call-start = ((), (), s32[]{:S(2)}) async-start(), calls=%async_computation.43 | async-start | bytes 7077888 | tf_op jit(solution)/shard_map/reduce_scatter | solution.py:279
  1395.4 247.9 %reduce-scatter.42.cloned.1.call-start = ((), (), s32[]{:S(2)}) async-start(), calls=%async_computation.44 | async-start | bytes 7077888 | tf_op jit(solution)/shard_map/reduce_scatter | solution.py:282
  1433.7 274.4 %reduce-scatter.44.cloned.1.call-start = ((), (), s32[]{:S(2)}) async-start(), calls=%async_computation.45 | async-start | bytes 7077888 | tf_op jit(solution)/shard_map/reduce_scatter | solution.py:285
  1472.7 529.8 %all-reduce.25.cloned.1.call-start = ((), (), s32[]{:S(2)}) async-start(), calls=%async_computation.50 | async-start | bytes 16777216 | tf_op jit(solution)/shard_map/psum | solution.py:122
  1580.6 421.9 %copy-start.200 = (f32[256]{0:T(256)S(1)}, f32[256]{0:T(256)}, u32[]{:S(2)}) copy-start(f32[256]{0:T(256)} %copy-done.198) | copy-start | bytes 3076
  (271 other events, 1533.3 us)
Sparse Core Ops, SparseCore 0:
  9.9 26.0 all-gather.23
  37.9 23.3 all-gather.27
  63.2 27.7 all-gather.31
  93.3 23.3 all-gather.45
  119.0 23.4 all-gather.47
  144.3 28.0 all-gather.33
  175.9 51.8 all-reduce.22
  235.3 22.7 all-gather.51
  260.0 23.3 all-gather.49
  285.1 23.3 all-gather.25
  310.4 23.3 all-gather.41
  335.5 45.3 all-gather.35
  382.8 46.5 all-gather.39
  431.2 45.3 all-gather.37
  478.3 23.4 all-gather.29
  503.6 23.5 all-gather.43
  528.5 80.7 all-gather.57
  612.9 119.5 all-reduce.26
  759.4 79.7 all-gather.55
  840.6 79.2 all-gather.59
  921.4 79.2 all-gather.53
  1035.5 34.4 reduce-scatter.23
  1073.1 35.9 reduce-scatter.15
  1112.2 35.9 reduce-scatter.27
  1151.3 35.9 reduce-scatter.19
  1191.0 35.9 reduce-scatter.17
  1230.0 35.9 reduce-scatter.21
  1269.2 35.9 reduce-scatter.25
  1308.9 35.9 reduce-scatter.29
  1348.0 41.1 reduce-scatter.31
  1392.4 35.9 reduce-scatter.33
  1432.1 35.9 reduce-scatter.35
  1471.2 41.1 reduce-scatter.37
  1516.4 61.7 reduce-scatter.39
  1581.5 61.7 reduce-scatter.41
  1646.5 61.5 reduce-scatter.43
  1711.4 291.0 all-reduce.24
